TPU v7x, 32 devices: a whole 2x2x4 slice. The times are simulated.
32 devices in a mesh: seq: 16 (over z, y, x), tp: 2 (over core).
Axes of the slice: x: 2, y: 2, z: 4, core: 2. Of those that a mesh axis runs over, the one named last changes fastest.
Arguments:
- img: bfloat16 [4, 512, 3072], P(None, 'seq', 'tp'), may hold values from -6 to 6
- txt: bfloat16 [4, 64, 3072], P(None, 'seq', 'tp'), may hold values from -6 to 6
- prev_mod: bfloat16 [4, 512, 3072], P(None, 'seq', 'tp'), may hold values from -47 to 47
- cache: float32 [4, 512, 3072], P(None, 'seq', 'tp'), may hold values from -6 to 6
- modulation: bfloat16 [3, 4, 3072], P(None, None, 'tp'), may hold values from -4 to 4
- w_qkv: bfloat16 [3072, 3, 2048], P('seq', None, 'tp'), may hold values from -1 to 1, as said below
- qk_gain: float32 [2, 2048], P(None, 'tp'), may hold values from 0.5 to 6, as said below
- output_weight: bfloat16 [2048, 3072], P('tp'), may hold values from -0.1875 to 0.1875
- text_len: int32 [4], replicated, may hold values from 1 to 64
- refresh: int32 [4], replicated, may hold values from 0 to 1, as said below
Outputs:
- out_img: float32 [4, 512, 3072], P(None, 'seq', 'tp')
- new_cache: float32 [4, 512, 3072], P(None, 'seq', 'tp')
- rel_l1: float32 [4], replicated
Inputs may be any that keep to these rules, and one draw needn't show every extreme that they name: `refresh`: at least one sequence has flag 1 and at least one has flag 0. `w_qkv`: entries of spread about one over the square root of 3072. `qk_gain`: positive.
All inputs are finite; a program needn't handle non-finite values.
Results may differ from a plain program's by a relative error of at most 0.013.
The roundings to bfloat16 on the way count: a program that leaves them out, or rounds other values in their place, can miss the bound.
Values may be sent and summed in bfloat16 or wider, within the bound.
A program may use at most 128 MiB of HBM per device.

v0:
```python
import jax
import jax.numpy as jnp
from jax import lax
from jax.sharding import PartitionSpec as P

HD = 128
EPS = 0.1
NEG = -1e30


def unit_heads(block, gain):
    shaped = block.reshape(block.shape[:-1] + (block.shape[-1] // HD, HD))
    scaled = shaped * lax.rsqrt(jnp.mean(jnp.square(shaped), axis=-1, keepdims=True) + EPS)
    return scaled.reshape(block.shape) * gain


def local(img, txt, prev_mod, cache, modulation, w_qkv, qk_gain, output_weight, text_len, refresh):
    batch, img_rows, width_loc = img.shape
    txt_rows = txt.shape[1]
    rows = txt_rows + img_rows
    joined = jnp.concatenate([txt, img], axis=1)
    local_mods = modulation.astype(jnp.float32)
    wide, wide_mod = (
        lax.all_gather(joined, "tp", axis=2, tiled=True),
        lax.all_gather(modulation, "tp", axis=2, tiled=True),
    )
    wide_mods = wide_mod.astype(jnp.float32)
    values = wide.astype(jnp.float32)
    center = jnp.mean(values, axis=2, keepdims=True)
    spread = jnp.mean(jnp.square(values - center), axis=2, keepdims=True)
    normed = (values - center) * lax.rsqrt(spread + EPS)
    modded = (normed * (1.0 + wide_mods[1][:, None, :]) + wide_mods[0][:, None, :]).astype(
        jnp.bfloat16
    )
    offset = lax.axis_index("tp") * width_loc
    own_image = lax.dynamic_slice_in_dim(modded[:, txt_rows:, :], offset, width_loc, 2)
    previous = prev_mod.astype(jnp.float32)
    gap = jnp.sum(jnp.abs(own_image.astype(jnp.float32) - previous), axis=(1, 2))
    base_sum = jnp.sum(jnp.abs(previous), axis=(1, 2))
    numer, denom = lax.psum((gap, base_sum), ("seq", "tp"))
    rel_l1 = numer / jnp.maximum(denom, 1.0)
    columns = w_qkv.shape[2]
    projected = jnp.einsum(
        "btd,dkc->btkc",
        modded,
        lax.all_gather(w_qkv, "seq", axis=0, tiled=True),
        preferred_element_type=jnp.float32,
    )
    heads = columns // HD
    query = unit_heads(projected[:, txt_rows:, 0, :], qk_gain[0]).astype(jnp.bfloat16)
    query_heads = query.reshape(batch, img_rows, heads, HD)
    keyed = unit_heads(projected[:, :, 1, :], qk_gain[1]).astype(jnp.bfloat16)
    valued = projected[:, :, 2, :].astype(jnp.bfloat16)
    paired = jnp.stack([keyed, valued], axis=2)
    score_scale = 1.0 / HD**0.5
    start_top = jnp.full((batch, heads, img_rows), NEG, jnp.float32)
    piece = lax.all_gather(paired, "seq", axis=1, tiled=True)
    top = start_top
    count = piece.shape[1]
    index = jnp.arange(count, dtype=jnp.int32)
    slot = index % rows
    text_pos = index // rows * txt_rows + slot
    valid = (slot >= txt_rows)[None, :] | (text_pos[None, :] < text_len[:, None])
    keys = piece[:, :, 0, :].reshape(batch, count, heads, HD)
    vals = piece[:, :, 1, :].reshape(batch, count, heads, HD)
    logit_scores = (
        jnp.einsum("bqhc,bkhc->bhqk", query_heads, keys, preferred_element_type=jnp.float32)
        * score_scale
    )
    logit_scores = jnp.where(valid[:, None, None, :], logit_scores, NEG)
    new_top = jnp.maximum(top, jnp.max(logit_scores, axis=3))
    attention_weights = jnp.where(
        valid[:, None, None, :], jnp.exp(logit_scores - new_top[..., None]), 0.0
    )
    total = jnp.sum(attention_weights, axis=3)
    summed_output = jnp.einsum(
        "bhqk,bkhc->bhqc",
        attention_weights.astype(jnp.bfloat16),
        vals,
        preferred_element_type=jnp.float32,
    )
    top, total, summed_output = (new_top, total, summed_output)
    attended_values = (summed_output / total[..., None]).astype(jnp.bfloat16)
    attended_values = attended_values.transpose(0, 2, 1, 3).reshape(batch, img_rows, columns)
    partial_output = jnp.einsum(
        "pxr,ro->pxo", attended_values, output_weight, preferred_element_type=jnp.float32
    )
    whole = lax.psum(partial_output.astype(jnp.bfloat16), "tp").astype(jnp.float32)
    mixed_heads = lax.dynamic_slice_in_dim(whole, lax.axis_index("tp") * width_loc, width_loc, 2)
    resid = local_mods[2][:, None, :] * mixed_heads
    flag = (refresh == 1)[:, None, None]
    new_cache = jnp.where(flag, resid, cache)
    out_img = img.astype(jnp.float32) + new_cache
    return (out_img, new_cache, rel_l1)


def solution(mesh):
    return jax.shard_map(
        local,
        mesh=mesh,
        in_specs=(
            P(None, "seq", "tp"),
            P(None, "seq", "tp"),
            P(None, "seq", "tp"),
            P(None, "seq", "tp"),
            P(None, None, "tp"),
            P("seq", None, "tp"),
            P(None, "tp"),
            P("tp", None),
            P(),
            P(),
        ),
        out_specs=(P(None, "seq", "tp"), P(None, "seq", "tp"), P()),
        check_vma=False,
    )
```

profile of v0, /device:TPU:0, one launch (start us, length us, event | category | flops | bytes accessed | tf_op | source)
XLA Modules:
  0.0 434.7 jit_solution(10169232465015273428)
XLA Ops:
  7.2 0.7 all-gather.3.cloned.1.call-update
  8.0 2.2 all_gather.13
  10.2 1.1 pad_maximum_fusion.1
  11.3 2.5 all_gather.12
  14.1 0.4 fusion.14
  14.5 0.5 fusion.17
  15.0 209.3 %all-gather.3.cloned.1.call-done = bf16[3072,3,1024]{2,0,1:T(8,128)(2,1)} async-done(((bf16[192,3,1024]{2,0,1:T(8,128)(2,1)}), bf16[3072,3,1024]{2,0,1:T(8,128)(2,1)}) %all-gather.3.cloned.1.call-update) | async-done | bytes 18874384 | tf_op jit(solution)/shard_map/all_gather | solution.py:46
  224.3 8.1 %fusion = f32[4,36,3,1024]{3,1,2,0:T(8,128)S(1)} fusion(bf16[3072,3,1024]{2,0,1:T(8,128)(2,1)} %all-gather.3.cloned.1.call-done, bf16[4,36,3072]{2,1,0:T(8,128)(2,1)S(1)} %fusion.17), kind=kOutput, calls=%fused_computation | convolution fusion | flops 2717908992 | bytes 21528576 | tf_op jit(solution)/shard_map/btd,dkc->btkc/dot_general | solution.py:43
  232.4 0.9 slice_multiply_fusion
  233.3 0.8 slice.62
  234.1 1.2 reshape.130
  235.3 0.9 reduce_sum.66
  236.1 1.0 copy.47
  237.2 1.0 mul.103
  238.3 1.3 mul.104
  239.9 1.1 pad_maximum_fusion
  241.0 1.3 copy.50
  242.4 1.1 slice.53
  243.5 1.3 fusion.49
  244.8 40.5 %all-reduce = (f32[4]{0:T(128)S(1)}, f32[4]{0:T(128)S(1)}) all-reduce(f32[4]{0:T(128)S(1)} %get-tuple-element.4, f32[4]{0:T(128)S(1)} %get-tuple-element.3), channel_id=1, replica_groups=mesh['seq'=16,'tp'=2] {'seq','tp'}, use_global_device_ids=true, to_apply=%region_8.9 | all-reduce | flops 8 | bytes 64 | tf_op jit(solution)/shard_map/psum | solution.py:40
  286.0 77.3 %all-gather.5.cloned.1.call-done = bf16[4,576,2,1024]{3,0,2,1:T(4,128)(2,1)} async-done(((bf16[4,36,2,1024]{3,0,2,1:T(4,128)(2,1)}), bf16[4,576,2,1024]{3,0,2,1:T(4,128)(2,1)}) %all-gather.5.cloned.1.call-update) | async-done | bytes 9437200 | tf_op jit(solution)/shard_map/all_gather | solution.py:57
  363.3 10.7 %fusion.70 = (bf16[4,576,1,1024]{3,0,2,1:T(4,128)(2,1)}, bf16[4,576,1,1024]{3,0,2,1:T(4,128)(2,1)}) fusion(bf16[4,576,2,1024]{3,0,2,1:T(4,128)(2,1)} %all-gather.5.cloned.1.call-done), kind=kLoop, calls=%fused_computation.82 | loop fusion | bytes 18874368 | tf_op jit(solution)/shard_map/slice | solution.py:64
  374.0 8.0 %reshape.131 = bf16[4,576,8,128]{3,2,0,1:T(8,128)(2,1)} reshape(bf16[4,576,1,1024]{3,0,2,1:T(4,128)(2,1)} %get-tuple-element.9) | data formatting | bytes 9437184 | tf_op jit(solution)/shard_map/reshape;squeeze | solution.py:64
  382.0 7.5 %fusion.13 = (f32[4,8,32]{2,1,0:T(8,128)S(1)}, f32[4,8,32,576]{3,2,1,0:T(8,128)S(1)}) fusion(pred[4,576]{1,0:T(4,128)(4,1)S(1)} %compare_or_fusion, bf16[4,576,8,128]{3,2,0,1:T(8,128)(2,1)} %reshape.131, bf16[4,32,8,128]{3,2,1,0:T(8,128)(2,1)S(1)} %fusion.54), kind=kOutput, calls=%fused_computation.15 | convolution fusion | flops 152763392 | bytes 7346432 | tf_op jit(solution)/shard_map/bqhc,bkhc->bhqk/dot_general | solution.py:67
  389.5 8.0 %reshape.132 = bf16[4,576,8,128]{3,2,0,1:T(8,128)(2,1)} reshape(bf16[4,576,1,1024]{3,0,2,1:T(4,128)(2,1)} %get-tuple-element.10) | data formatting | bytes 9437184 | tf_op jit(solution)/shard_map/reshape;squeeze | solution.py:65
  397.6 0.8 fusion.18
  398.4 8.1 %fusion.41 = bf16[4,8,4,8,128]{4,3,2,1,0:T(8,128)(2,1)S(1)} fusion(bf16[4,576,8,128]{3,2,0,1:T(8,128)(2,1)} %reshape.132, f32[4,8,32,576]{3,2,1,0:T(8,128)S(1)} %get-tuple-element.16, f32[4,8,32]{2,1,0:T(8,128)S(1)} %broadcast_maximum_fusion, pred[4,576]{1,0:T(4,128)(4,1)S(1)} %compare_or_fusion, f32[4,32,8]{1,2,0:T(8,128)S(1)} %bitcast.67), kind=kOutput, calls=%fused_computation.30 | convolution fusion | flops 154206208 | bytes 7350528 | tf_op jit(solution)/shard_map/bhqk,bkhc->bhqc/dot_general | solution.py:76
  406.6 1.9 fusion.8
  408.5 0.5 maximum_divide_fusion
  409.0 0.7 bitcast_convert_fusion
  409.7 16.1 %all-reduce.3.cloned.1.call-done = bf16[4,32,3072]{2,1,0:T(8,128)(2,1)} async-done(((bf16[4,32,3072]{2,1,0:T(8,128)(2,1)}), bf16[4,32,3072]{2,1,0:T(8,128)(2,1)}) %all-reduce.3.cloned.1.call-update) | async-done | bytes 786448 | tf_op jit(solution)/shard_map/psum | solution.py:88
  425.8 2.4 convert_add_fusion
  (41 shorter events, 1.7 us)
Async XLA Ops:
  7.2 217.1 %all-gather.3.cloned.1.call-start = ((), (), s32[]{:S(2)}) async-start(), calls=%async_computation | async-start | bytes 20054016 | tf_op jit(solution)/shard_map/all_gather | solution.py:46
  7.9 6.6 %copy-start.3 = (f32[2,1024]{1,0:T(2,128)S(1)}, f32[2,1024]{1,0:T(2,128)}, u32[]{:S(2)}) copy-start(f32[2,1024]{1,0:T(2,128)} %param.16) | copy-start | bytes 24580
  7.9 355.4 %all-gather.5.cloned.1.call-start = ((), (), s32[]{:S(2)}) async-start(), calls=%async_computation.1 | async-start | bytes 10027008 | tf_op jit(solution)/shard_map/all_gather | solution.py:57
  239.9 3.6 copy-start.2
  239.9 45.4 %copy-start.4 = (s32[4]{0:T(128)S(1)}, s32[4]{0:T(128)}, u32[]{:S(2)}) copy-start(s32[4]{0:T(128)} %param.18) | copy-start | bytes 52
  242.3 183.5 %all-reduce.3.cloned.1.call-start = ((), (), s32[]{:S(2)}) async-start(), calls=%async_computation.2 | async-start | bytes 1572864 | tf_op jit(solution)/shard_map/psum | solution.py:88
  397.6 8.9 %slice-start = ((s8[6291456]{0:T(1024)(128)(4,1)}), s8[4194304]{0:T(1024)(128)(4,1)S(1)}, s32[]{:S(2)}) async-start(s8[6291456]{0:T(1024)(128)(4,1)} %bitcast.62), calls=%async_computation.3 | async-start | bytes 8388608
  398.4 8.1 %slice-start.1 = ((s8[6291456]{0:T(1024)(128)(4,1)}), s8[2097152]{0:T(1024)(128)(4,1)S(1)}, s32[]{:S(2)}) async-start(s8[6291456]{0:T(1024)(128)(4,1)} %bitcast.62), calls=%async_computation.4 | async-start | bytes 4194304
  406.5 1.9 copy-start.5
  406.5 19.2 %copy-start = (bf16[4,32,1536]{2,1,0:T(8,128)(2,1)S(1)}, bf16[4,32,1536]{2,1,0:T(8,128)(2,1)}, u32[]{:S(2)}) copy-start(bf16[4,32,1536]{2,1,0:T(8,128)(2,1)} %param.10) | copy-start | bytes 1179652
  406.6 19.2 %copy-start.1 = (f32[4,32,1536]{2,1,0:T(8,128)S(1)}, f32[4,32,1536]{2,1,0:T(8,128)}, u32[]{:S(2)}) copy-start(f32[4,32,1536]{2,1,0:T(8,128)} %param.13) | copy-start | bytes 2359300
Sparse Core Ops, SparseCore 0:
  10.6 213.6 all-gather.2
  242.4 120.8 all-gather.4
  408.6 17.1 all-reduce.2
where the time goes:
time: 436 us; the launch traced here: 435 us
  waiting for transfers between devices  303 us (69%)
  blocking collectives  45.3 us (10%)
  local copies, waits for them, and re-layouts  34.7 us (8%)
  matrix products  25.6 us (6%)
  between operations  14 us (3%)
  other arithmetic  11.8 us (3%)
    all_gather x1, waiting for transfers between devices, local(): lax.all_gather(w_qkv, 'seq', axis=0, tiled=True)  209 us
    all_gather x1, waiting for transfers between devices, local(): piece = lax.all_gather(paired, 'seq', axis=1, tiled=True)  77.3 us
    psum x1, blocking collectives, local(): numer, denom = lax.psum((gap, base_sum), ('seq', 'tp'))  40.5 us
    psum x1, waiting for transfers between devices, local(): lax.psum(partial_output.astype(jnp.bfloat16), 'tp').astype(jnp.float32)  16.1 us
    slice x1, local copies, waits for them, and re-layouts, local(): keys = piece[:, :, 0, :].reshape(batch, count, heads, HD)  10.7 us
  transfers between devices with their start and end apart: 3, of which 3 were waited for; matrix products, arithmetic and copies ran while one was open for 2% of the time, Pallas kernels for 0%

commit v1 on v0

--- a/solution.py
+++ b/solution.py
@@ -54,7 +54,12 @@
     paired = jnp.stack([keyed, valued], axis=2)
     score_scale = 1.0 / HD**0.5
     start_top = jnp.full((batch, heads, img_rows), NEG, jnp.float32)
-    piece = lax.all_gather(paired, "seq", axis=1, tiled=True)
+    ring = [paired]
+    for hop in range(15):
+        ring.append(lax.ppermute(ring[-1], "seq", [(dev, (dev + 1) % 16) for dev in range(16)]))
+    piece = jnp.roll(
+        jnp.concatenate(ring[::-1], axis=1), (lax.axis_index("seq") + 1) * ring[0].shape[1], axis=1
+    )
     top = start_top
     count = piece.shape[1]
     index = jnp.arange(count, dtype=jnp.int32)

time: 436 us -> 709 us (1.63)
  local copies, waits for them, and re-layouts: 34.7 us -> 176 us
  waiting for transfers between devices: 303 us -> 438 us
  matrix products: 25.6 us -> 13.5 us
    ppermute x0 -> x15, waiting for transfers between devices: none -> 210 us  [local(): lax.ppermute(ring[-1], 'seq', [(dev, (dev + 1) % 16) for dev in range(16)])]
    concatenate x0 -> x1, local copies, waits for them, and re-layouts: none -> 134 us  [local(): jnp.roll(jnp.concatenate(ring[::-1], axis=1), (lax.axis_index('seq') + 1)...]
    all_gather x1 -> x0, waiting for transfers between devices: 77.3 us -> none  [local(): piece = lax.all_gather(paired, 'seq', axis=1, tiled=True)]
    ppermute x0 -> x15, local copies, waits for them, and re-layouts: none -> 16.5 us  [local(): lax.ppermute(ring[-1], 'seq', [(dev, (dev + 1) % 16) for dev in range(16)])]
    another operation x2 -> x0, local copies, waits for them, and re-layouts: 16.1 us -> none  [the longest x1 8.05 us: local(): vals = piece[:, :, 1, :].reshape(batch, count, heads, HD)]
    unnamed x17 -> x73, local copies, waits for them, and re-layouts: 0.14 us -> 13 us
  transfers between devices with their start and end apart: 3 -> 17, of which waited for: 3 -> 16; matrix products, arithmetic and copies ran while one was open for 2% -> 3% of each run, Pallas kernels for 0% -> 0%
where the time goes in v1:
time: 709 us; the launch traced here: 703 us
  waiting for transfers between devices  438 us (62%)
  local copies, waits for them, and re-layouts  176 us (25%)
  blocking collectives  44.7 us (6%)
  between operations  14.5 us (2%)
  matrix products  13.5 us (2%)
  other arithmetic  11.9 us (2%)
    ppermute x15, waiting for transfers between devices, local(): lax.ppermute(ring[-1], 'seq', [(dev, (dev + 1) % 16) for dev in range(16)])  210 us
    all_gather x1, waiting for transfers between devices, local(): lax.all_gather(w_qkv, 'seq', axis=0, tiled=True)  209 us
    concatenate x1, local copies, waits for them, and re-layouts, local(): jnp.roll(jnp.concatenate(ring[::-1], axis=1), (lax.axis_index('seq') + 1)...  134 us
    psum x1, blocking collectives, local(): numer, denom = lax.psum((gap, base_sum), ('seq', 'tp'))  40 us
    psum x1, waiting for transfers between devices, local(): lax.psum(partial_output.astype(jnp.bfloat16), 'tp').astype(jnp.float32)  17.6 us
    ppermute x15, local copies, waits for them, and re-layouts, local(): lax.ppermute(ring[-1], 'seq', [(dev, (dev + 1) % 16) for dev in range(16)])  16.5 us
  transfers between devices with their start and end apart: 17, of which 16 were waited for; matrix products, arithmetic and copies ran while one was open for 3% of the time, Pallas kernels for 0%

profile of v1, /device:TPU:0, one launch (start us, length us, event | category | flops | bytes accessed | tf_op | source)
XLA Modules:
  0.0 703.1 jit_solution(5250217931778651678)
XLA Ops:
  8.0 2.2 all_gather.10
  11.3 2.5 all_gather.9
  15.0 209.3 %all-gather.2.cloned.1.call-done = bf16[3072,3,1024]{2,0,1:T(8,128)(2,1)} async-done(((bf16[192,3,1024]{2,0,1:T(8,128)(2,1)}), bf16[3072,3,1024]{2,0,1:T(8,128)(2,1)}) %all-gather.2.cloned.1.call-update) | async-done | bytes 18874384 | tf_op jit(solution)/shard_map/all_gather | solution.py:46
  224.3 8.1 %fusion = f32[4,36,3,1024]{3,1,2,0:T(8,128)S(1)} fusion(bf16[3072,3,1024]{2,0,1:T(8,128)(2,1)} %all-gather.2.cloned.1.call-done, bf16[4,36,3072]{2,1,0:T(8,128)(2,1)S(1)} %fusion.17), kind=kOutput, calls=%fused_computation | convolution fusion | flops 2717908992 | bytes 21528576 | tf_op jit(solution)/shard_map/btd,dkc->btkc/dot_general | solution.py:43
  238.3 1.3 mul.107
  242.3 1.5 collective-permute-start
  243.8 16.5 %collective-permute-done = bf16[4,36,2,1024]{3,0,2,1:T(4,128)(2,1)S(1)} collective-permute-done((bf16[4,36,2,1024]{3,0,2,1:T(4,128)(2,1)S(1)}, bf16[4,36,2,1024]{3,0,2,1:T(4,128)(2,1)S(1)}, u32[]{:S(2)}, u32[]{:S(2)}) %collective-permute-start) | collective-permute-done | bytes 589856 | tf_op jit(solution)/shard_map/ppermute | solution.py:59
  261.1 17.1 %collective-permute-done.1 = bf16[4,36,2,1024]{3,0,2,1:T(4,128)(2,1)S(1)} collective-permute-done((bf16[4,36,2,1024]{3,0,2,1:T(4,128)(2,1)S(1)}, bf16[4,36,2,1024]{3,0,2,1:T(4,128)(2,1)S(1)}, u32[]{:S(2)}, u32[]{:S(2)}) %collective-permute-start.1) | collective-permute-done | bytes 589856 | tf_op jit(solution)/shard_map/ppermute | solution.py:59
  279.0 16.2 %collective-permute-done.2 = bf16[4,36,2,1024]{3,0,2,1:T(4,128)(2,1)S(1)} collective-permute-done((bf16[4,36,2,1024]{3,0,2,1:T(4,128)(2,1)S(1)}, bf16[4,36,2,1024]{3,0,2,1:T(4,128)(2,1)S(1)}, u32[]{:S(2)}, u32[]{:S(2)}) %collective-permute-start.2) | collective-permute-done | bytes 589856 | tf_op jit(solution)/shard_map/ppermute | solution.py:59
  296.1 15.4 %collective-permute-done.3 = bf16[4,36,2,1024]{3,0,2,1:T(4,128)(2,1)S(1)} collective-permute-done((bf16[4,36,2,1024]{3,0,2,1:T(4,128)(2,1)S(1)}, bf16[4,36,2,1024]{3,0,2,1:T(4,128)(2,1)S(1)}, u32[]{:S(2)}, u32[]{:S(2)}) %collective-permute-start.3) | collective-permute-done | bytes 589856 | tf_op jit(solution)/shard_map/ppermute | solution.py:59
  312.3 14.5 %collective-permute-done.4 = bf16[4,36,2,1024]{3,0,2,1:T(4,128)(2,1)S(1)} collective-permute-done((bf16[4,36,2,1024]{3,0,2,1:T(4,128)(2,1)S(1)}, bf16[4,36,2,1024]{3,0,2,1:T(4,128)(2,1)S(1)}, u32[]{:S(2)}, u32[]{:S(2)}) %collective-permute-start.4) | collective-permute-done | bytes 589856 | tf_op jit(solution)/shard_map/ppermute | solution.py:59
  327.6 13.7 %collective-permute-done.5 = bf16[4,36,2,1024]{3,0,2,1:T(4,128)(2,1)S(1)} collective-permute-done((bf16[4,36,2,1024]{3,0,2,1:T(4,128)(2,1)S(1)}, bf16[4,36,2,1024]{3,0,2,1:T(4,128)(2,1)S(1)}, u32[]{:S(2)}, u32[]{:S(2)}) %collective-permute-start.5) | collective-permute-done | bytes 589856 | tf_op jit(solution)/shard_map/ppermute | solution.py:59
  342.2 13.6 %collective-permute-done.6 = bf16[4,36,2,1024]{3,0,2,1:T(4,128)(2,1)S(1)} collective-permute-done((bf16[4,36,2,1024]{3,0,2,1:T(4,128)(2,1)S(1)}, bf16[4,36,2,1024]{3,0,2,1:T(4,128)(2,1)S(1)}, u32[]{:S(2)}, u32[]{:S(2)}) %collective-permute-start.6) | collective-permute-done | bytes 589856 | tf_op jit(solution)/shard_map/ppermute | solution.py:59
  356.6 14.8 %collective-permute-done.7 = bf16[4,36,2,1024]{3,0,2,1:T(4,128)(2,1)S(1)} collective-permute-done((bf16[4,36,2,1024]{3,0,2,1:T(4,128)(2,1)S(1)}, bf16[4,36,2,1024]{3,0,2,1:T(4,128)(2,1)S(1)}, u32[]{:S(2)}, u32[]{:S(2)}) %collective-permute-start.7) | collective-permute-done | bytes 589856 | tf_op jit(solution)/shard_map/ppermute | solution.py:59
  372.2 15.9 %collective-permute-done.8 = bf16[4,36,2,1024]{3,0,2,1:T(4,128)(2,1)S(1)} collective-permute-done((bf16[4,36,2,1024]{3,0,2,1:T(4,128)(2,1)S(1)}, bf16[4,36,2,1024]{3,0,2,1:T(4,128)(2,1)S(1)}, u32[]{:S(2)}, u32[]{:S(2)}) %collective-permute-start.8) | collective-permute-done | bytes 589856 | tf_op jit(solution)/shard_map/ppermute | solution.py:59
  389.0 17.1 %collective-permute-done.9 = bf16[4,36,2,1024]{3,0,2,1:T(4,128)(2,1)S(1)} collective-permute-done((bf16[4,36,2,1024]{3,0,2,1:T(4,128)(2,1)S(1)}, bf16[4,36,2,1024]{3,0,2,1:T(4,128)(2,1)S(1)}, u32[]{:S(2)}, u32[]{:S(2)}) %collective-permute-start.9) | collective-permute-done | bytes 589856 | tf_op jit(solution)/shard_map/ppermute | solution.py:59
  406.9 18.2 %collective-permute-done.10 = bf16[4,36,2,1024]{3,0,2,1:T(4,128)(2,1)S(1)} collective-permute-done((bf16[4,36,2,1024]{3,0,2,1:T(4,128)(2,1)S(1)}, bf16[4,36,2,1024]{3,0,2,1:T(4,128)(2,1)S(1)}, u32[]{:S(2)}, u32[]{:S(2)}) %collective-permute-start.10) | collective-permute-done | bytes 589856 | tf_op jit(solution)/shard_map/ppermute | solution.py:59
  425.9 19.4 %collective-permute-done.11 = bf16[4,36,2,1024]{3,0,2,1:T(4,128)(2,1)S(1)} collective-permute-done((bf16[4,36,2,1024]{3,0,2,1:T(4,128)(2,1)S(1)}, bf16[4,36,2,1024]{3,0,2,1:T(4,128)(2,1)S(1)}, u32[]{:S(2)}, u32[]{:S(2)}) %collective-permute-start.11) | collective-permute-done | bytes 589856 | tf_op jit(solution)/shard_map/ppermute | solution.py:59
  446.4 17.7 %collective-permute-done.12 = bf16[4,36,2,1024]{3,0,2,1:T(4,128)(2,1)} collective-permute-done((bf16[4,36,2,1024]{3,0,2,1:T(4,128)(2,1)S(1)}, bf16[4,36,2,1024]{3,0,2,1:T(4,128)(2,1)}, u32[]{:S(2)}, u32[]{:S(2)}) %collective-permute-start.12) | collective-permute-done | bytes 589856 | tf_op jit(solution)/shard_map/ppermute | solution.py:59
  464.2 1.4 fusion.49
  465.6 40.0 %all-reduce = (f32[4]{0:T(128)}, f32[4]{0:T(128)}) all-reduce(f32[4]{0:T(128)S(1)} %get-tuple-element.4, f32[4]{0:T(128)S(1)} %get-tuple-element.3), channel_id=1, replica_groups=mesh['seq'=16,'tp'=2] {'seq','tp'}, use_global_device_ids=true, to_apply=%region_8.9 | all-reduce | flops 8 | bytes 64 | tf_op jit(solution)/shard_map/psum | solution.py:40
  505.9 2.5 collective-permute-start.14
  519.8 2.3 copy.104
  522.1 2.2 copy.103
  525.6 133.6 %concatenate.10 = bf16[4,1152,2,1024]{3,1,2,0:T(8,128)(2,1)} concatenate(bf16[4,36,2,1024]{3,1,2,0:T(8,128)(2,1)} %copy.102, bf16[4,36,2,1024]{3,1,2,0:T(8,128)(2,1)} %copy.103, bf16[4,36,2,1024]{3,1,2,0:T(8,128)(2,1)} %copy.104, bf16[4,36,2,1024]{3,1,2,0:T(8,128)(2,1)} %copy.105, bf16[4,36,2,1024]{3,1,2,0:T(8,128)(2,1)} %copy.106, bf16[4,36,2,1024]{3,1,2,0:T(8,128)(2,1)} %copy.107, ...), dimensions={1} | concatenate | bytes 37748736 | tf_op jit(solution)/shard_map/jit(_roll_dynamic)/concatenate | solution.py:60
  659.2 6.5 constant_dynamic-slice_fusion
  667.0 1.7 fusion.13
  668.7 1.2 copy.143
  670.8 1.8 fusion.41
  673.1 1.9 fusion.8
  676.2 17.6 %all-reduce.3.cloned.1.call-done = bf16[4,32,3072]{2,1,0:T(8,128)(2,1)} async-done(((bf16[4,32,3072]{2,1,0:T(8,128)(2,1)}), bf16[4,32,3072]{2,1,0:T(8,128)(2,1)}) %all-reduce.3.cloned.1.call-update) | async-done | bytes 786448 | tf_op jit(solution)/shard_map/psum | solution.py:93
  693.8 2.4 convert_add_fusion
  (138 shorter events, 38.4 us)
Async XLA Ops:
  7.2 217.1 %all-gather.2.cloned.1.call-start = ((), (), s32[]{:S(2)}) async-start(), calls=%async_computation | async-start | bytes 20054016 | tf_op jit(solution)/shard_map/all_gather | solution.py:46
  7.9 6.6 copy-start.28
  7.9 685.9 %all-reduce.3.cloned.1.call-start = ((), (), s32[]{:S(2)}) async-start(), calls=%async_computation.1 | async-start | bytes 1572864 | tf_op jit(solution)/shard_map/psum | solution.py:93
  239.9 265.7 %copy-start.29 = (s32[4]{0:T(128)S(1)}, s32[4]{0:T(128)}, u32[]{:S(2)}) copy-start(s32[4]{0:T(128)} %param.18) | copy-start | bytes 52
  242.3 18.0 %collective-permute-start = (bf16[4,36,2,1024]{3,0,2,1:T(4,128)(2,1)S(1)}, bf16[4,36,2,1024]{3,0,2,1:T(4,128)(2,1)S(1)}, u32[]{:S(2)}, u32[]{:S(2)}) collective-permute-start(bf16[4,36,2,1024]{3,0,2,1:T(4,128)(2,1)S(1)} %copy.101), channel_id=1, source_target_pairs={{0,2},{2,4},{4,6},{6,8},{8,10},{10,12},{12,14},{14,16},{16,18},{18... | collective-permute-start | bytes 1769480 | tf_op jit(solution)/shard_map/ppermute | solution.py:59
  261.1 17.1 %collective-permute-start.1 = (bf16[4,36,2,1024]{3,0,2,1:T(4,128)(2,1)S(1)}, bf16[4,36,2,1024]{3,0,2,1:T(4,128)(2,1)S(1)}, u32[]{:S(2)}, u32[]{:S(2)}) collective-permute-start(bf16[4,36,2,1024]{3,0,2,1:T(4,128)(2,1)S(1)} %collective-permute-done), channel_id=1, source_target_pairs={{0,2},{2,4},{4,6},{6,8},{8,10},{10,12},{12,14},{14,16},{16,18},{18... | collective-permute-start | bytes 1769480 | tf_op jit(solution)/shard_map/ppermute | solution.py:59
  279.0 16.2 %collective-permute-start.2 = (bf16[4,36,2,1024]{3,0,2,1:T(4,128)(2,1)S(1)}, bf16[4,36,2,1024]{3,0,2,1:T(4,128)(2,1)S(1)}, u32[]{:S(2)}, u32[]{:S(2)}) collective-permute-start(bf16[4,36,2,1024]{3,0,2,1:T(4,128)(2,1)S(1)} %collective-permute-done.1), channel_id=1, source_target_pairs={{0,2},{2,4},{4,6},{6,8},{8,10},{10,12},{12,14},{14,16},{16,18},{18... | collective-permute-start | bytes 1769480 | tf_op jit(solution)/shard_map/ppermute | solution.py:59
  296.1 15.4 %collective-permute-start.3 = (bf16[4,36,2,1024]{3,0,2,1:T(4,128)(2,1)S(1)}, bf16[4,36,2,1024]{3,0,2,1:T(4,128)(2,1)S(1)}, u32[]{:S(2)}, u32[]{:S(2)}) collective-permute-start(bf16[4,36,2,1024]{3,0,2,1:T(4,128)(2,1)S(1)} %collective-permute-done.2), channel_id=1, source_target_pairs={{0,2},{2,4},{4,6},{6,8},{8,10},{10,12},{12,14},{14,16},{16,18},{18... | collective-permute-start | bytes 1769480 | tf_op jit(solution)/shard_map/ppermute | solution.py:59
  312.3 14.5 %collective-permute-start.4 = (bf16[4,36,2,1024]{3,0,2,1:T(4,128)(2,1)S(1)}, bf16[4,36,2,1024]{3,0,2,1:T(4,128)(2,1)S(1)}, u32[]{:S(2)}, u32[]{:S(2)}) collective-permute-start(bf16[4,36,2,1024]{3,0,2,1:T(4,128)(2,1)S(1)} %collective-permute-done.3), channel_id=1, source_target_pairs={{0,2},{2,4},{4,6},{6,8},{8,10},{10,12},{12,14},{14,16},{16,18},{18... | collective-permute-start | bytes 1769480 | tf_op jit(solution)/shard_map/ppermute | solution.py:59
  327.6 13.7 %collective-permute-start.5 = (bf16[4,36,2,1024]{3,0,2,1:T(4,128)(2,1)S(1)}, bf16[4,36,2,1024]{3,0,2,1:T(4,128)(2,1)S(1)}, u32[]{:S(2)}, u32[]{:S(2)}) collective-permute-start(bf16[4,36,2,1024]{3,0,2,1:T(4,128)(2,1)S(1)} %collective-permute-done.4), channel_id=1, source_target_pairs={{0,2},{2,4},{4,6},{6,8},{8,10},{10,12},{12,14},{14,16},{16,18},{18... | collective-permute-start | bytes 1769480 | tf_op jit(solution)/shard_map/ppermute | solution.py:59
  342.1 13.6 %collective-permute-start.6 = (bf16[4,36,2,1024]{3,0,2,1:T(4,128)(2,1)S(1)}, bf16[4,36,2,1024]{3,0,2,1:T(4,128)(2,1)S(1)}, u32[]{:S(2)}, u32[]{:S(2)}) collective-permute-start(bf16[4,36,2,1024]{3,0,2,1:T(4,128)(2,1)S(1)} %collective-permute-done.5), channel_id=1, source_target_pairs={{0,2},{2,4},{4,6},{6,8},{8,10},{10,12},{12,14},{14,16},{16,18},{18... | collective-permute-start | bytes 1769480 | tf_op jit(solution)/shard_map/ppermute | solution.py:59
  356.6 14.8 %collective-permute-start.7 = (bf16[4,36,2,1024]{3,0,2,1:T(4,128)(2,1)S(1)}, bf16[4,36,2,1024]{3,0,2,1:T(4,128)(2,1)S(1)}, u32[]{:S(2)}, u32[]{:S(2)}) collective-permute-start(bf16[4,36,2,1024]{3,0,2,1:T(4,128)(2,1)S(1)} %collective-permute-done.6), channel_id=1, source_target_pairs={{0,2},{2,4},{4,6},{6,8},{8,10},{10,12},{12,14},{14,16},{16,18},{18... | collective-permute-start | bytes 1769480 | tf_op jit(solution)/shard_map/ppermute | solution.py:59
  372.2 15.9 %collective-permute-start.8 = (bf16[4,36,2,1024]{3,0,2,1:T(4,128)(2,1)S(1)}, bf16[4,36,2,1024]{3,0,2,1:T(4,128)(2,1)S(1)}, u32[]{:S(2)}, u32[]{:S(2)}) collective-permute-start(bf16[4,36,2,1024]{3,0,2,1:T(4,128)(2,1)S(1)} %collective-permute-done.7), channel_id=1, source_target_pairs={{0,2},{2,4},{4,6},{6,8},{8,10},{10,12},{12,14},{14,16},{16,18},{18... | collective-permute-start | bytes 1769480 | tf_op jit(solution)/shard_map/ppermute | solution.py:59
  389.0 17.1 %collective-permute-start.9 = (bf16[4,36,2,1024]{3,0,2,1:T(4,128)(2,1)S(1)}, bf16[4,36,2,1024]{3,0,2,1:T(4,128)(2,1)S(1)}, u32[]{:S(2)}, u32[]{:S(2)}) collective-permute-start(bf16[4,36,2,1024]{3,0,2,1:T(4,128)(2,1)S(1)} %collective-permute-done.8), channel_id=1, source_target_pairs={{0,2},{2,4},{4,6},{6,8},{8,10},{10,12},{12,14},{14,16},{16,18},{18... | collective-permute-start | bytes 1769480 | tf_op jit(solution)/shard_map/ppermute | solution.py:59
  406.9 18.2 %collective-permute-start.10 = (bf16[4,36,2,1024]{3,0,2,1:T(4,128)(2,1)S(1)}, bf16[4,36,2,1024]{3,0,2,1:T(4,128)(2,1)S(1)}, u32[]{:S(2)}, u32[]{:S(2)}) collective-permute-start(bf16[4,36,2,1024]{3,0,2,1:T(4,128)(2,1)S(1)} %collective-permute-done.9), channel_id=1, source_target_pairs={{0,2},{2,4},{4,6},{6,8},{8,10},{10,12},{12,14},{14,16},{16,18},{18... | collective-permute-start | bytes 1769480 | tf_op jit(solution)/shard_map/ppermute | solution.py:59
  425.9 19.4 %collective-permute-start.11 = (bf16[4,36,2,1024]{3,0,2,1:T(4,128)(2,1)S(1)}, bf16[4,36,2,1024]{3,0,2,1:T(4,128)(2,1)S(1)}, u32[]{:S(2)}, u32[]{:S(2)}) collective-permute-start(bf16[4,36,2,1024]{3,0,2,1:T(4,128)(2,1)S(1)} %collective-permute-done.10), channel_id=1, source_target_pairs={{0,2},{2,4},{4,6},{6,8},{8,10},{10,12},{12,14},{14,16},{16,18},{18... | collective-permute-start | bytes 1769480 | tf_op jit(solution)/shard_map/ppermute | solution.py:59
  445.3 18.9 %copy-start.26 = (bf16[4,36,2,1024]{3,0,2,1:T(4,128)(2,1)}, bf16[4,36,2,1024]{3,0,2,1:T(4,128)(2,1)S(1)}, u32[]{:S(2)}) copy-start(bf16[4,36,2,1024]{3,0,2,1:T(4,128)(2,1)S(1)} %collective-permute-done.11) | copy-start | bytes 1769476
  445.3 18.9 %collective-permute-start.12 = (bf16[4,36,2,1024]{3,0,2,1:T(4,128)(2,1)S(1)}, bf16[4,36,2,1024]{3,0,2,1:T(4,128)(2,1)}, u32[]{:S(2)}, u32[]{:S(2)}) collective-permute-start(bf16[4,36,2,1024]{3,0,2,1:T(4,128)(2,1)S(1)} %collective-permute-done.11), channel_id=1, source_target_pairs={{0,2},{2,4},{4,6},{6,8},{8,10},{10,12},{12,14},{14,16},{16,18},{18... | collective-permute-start | bytes 1769480 | tf_op jit(solution)/shard_map/ppermute | solution.py:59
  446.4 62.4 %copy-start.5 = (bf16[4,36,2,1024]{3,0,2,1:T(4,128)(2,1)S(1)}, bf16[4,36,2,1024]{3,0,2,1:T(4,128)(2,1)}, u32[]{:S(2)}) copy-start(bf16[4,36,2,1024]{3,0,2,1:T(4,128)(2,1)} %copy-done.4) | copy-start | bytes 1769476
  464.2 41.7 %collective-permute-start.13 = (bf16[4,36,2,1024]{3,0,2,1:T(4,128)(2,1)}, bf16[4,36,2,1024]{3,0,2,1:T(4,128)(2,1)}, u32[]{:S(2)}, u32[]{:S(2)}) collective-permute-start(bf16[4,36,2,1024]{3,0,2,1:T(4,128)(2,1)} %collective-permute-done.12), channel_id=1, source_target_pairs={{0,2},{2,4},{4,6},{6,8},{8,10},{10,12},{12,14},{14,16},{16,18},{18... | collective-permute-start | bytes 1769480 | tf_op jit(solution)/shard_map/ppermute | solution.py:59
  465.6 43.6 %copy-start.7 = (bf16[4,36,2,1024]{3,0,2,1:T(4,128)(2,1)S(1)}, bf16[4,36,2,1024]{3,0,2,1:T(4,128)(2,1)}, u32[]{:S(2)}) copy-start(bf16[4,36,2,1024]{3,0,2,1:T(4,128)(2,1)} %copy-done.6) | copy-start | bytes 1769476
  505.8 3.8 copy-start.9
  505.9 18.6 %collective-permute-start.14 = (bf16[4,36,2,1024]{3,0,2,1:T(4,128)(2,1)}, bf16[4,36,2,1024]{3,0,2,1:T(4,128)(2,1)S(1)}, u32[]{:S(2)}, u32[]{:S(2)}) collective-permute-start(bf16[4,36,2,1024]{3,0,2,1:T(4,128)(2,1)} %collective-permute-done.13), channel_id=1, source_target_pairs={{0,2},{2,4},{4,6},{6,8},{8,10},{10,12},{12,14},{14,16},{16,18},{18... | collective-permute-start | bytes 1769480 | tf_op jit(solution)/shard_map/ppermute | solution.py:59
  509.6 3.1 copy-start.17
  509.9 3.9 copy-start.19
  510.3 4.7 copy-start.21
  511.5 4.7 copy-start.23
  512.7 4.8 copy-start.25
  513.9 4.8 copy-start.27
  518.7 7.0 copy-start.1
  673.0 20.8 %copy-start.2 = (bf16[4,32,1536]{2,1,0:T(8,128)(2,1)S(1)}, bf16[4,32,1536]{2,1,0:T(8,128)(2,1)}, u32[]{:S(2)}) copy-start(bf16[4,32,1536]{2,1,0:T(8,128)(2,1)} %param.10) | copy-start | bytes 1179652
  673.0 20.8 %copy-start.3 = (f32[4,32,1536]{2,1,0:T(8,128)S(1)}, f32[4,32,1536]{2,1,0:T(8,128)}, u32[]{:S(2)}) copy-start(f32[4,32,1536]{2,1,0:T(8,128)} %param.13) | copy-start | bytes 2359300
  (20 other events, 25.9 us)
Sparse Core Ops, SparseCore 0:
  10.6 213.6 all-gather.1
  675.1 18.6 all-reduce.2
